TPU v7x, 256 devices: a 4x2x16 block of a 4x16x16 slice. The times are simulated.
256 devices in a mesh: clip: 2 (over y), tm: 16 (over z), space: 4 (over x), chan: 2 (over core).
Axes of the slice: x: 4, y: 2, z: 16, core: 2. Of those that a mesh axis runs over, the one named last changes fastest.
The devices are a block of a 4x16x16 slice.
Arguments:
- features: bfloat16 [64, 16, 90, 256], P(('clip', 'tm'), 'space'), parts along dimension 0, may hold values from -700 to 700
- hidden: bfloat16 [64, 16, 90, 256], P(('clip', 'tm'), 'space'), parts along dimension 0, may hold values from -700 to 700
- cotangent: bfloat16 [64, 16, 90, 256], P(('clip', 'tm'), 'space'), parts along dimension 0, may hold values from -6 to 6
- kernel_one: bfloat16 [256, 3, 3, 3, 256], P(None, None, None, None, 'chan'), may hold values from -0.078125 to 0.078125
- kernel_two: bfloat16 [256, 3, 3, 3, 256], P(None, None, None, None, 'chan'), may hold values from -0.078125 to 0.078125
- gains: float32 [2, 256], replicated, may hold values from 0.25 to 1.75
Outputs:
- feature_grad: bfloat16 [64, 16, 90, 256], P(('clip', 'tm'), 'space', None, 'chan'), parts along dimension 0
- delta_one: float32 [512, 3, 3, 3, 256], P(('clip', 'tm', 'space'), None, None, None, 'chan'), parts along dimension 0
- delta_two: float32 [512, 3, 3, 3, 256], P(('clip', 'tm', 'space'), None, None, None, 'chan'), parts along dimension 0
- gain_grads: float32 [4, 256], P('clip', 'chan'), parts along dimension 0
There are 2 independent parts, one for each index of `clip`. A program takes and returns all parts, laid end to end along the dimension named above; an argument that names none is the same for every part. Nothing has to cross between parts.
All inputs are finite; a program needn't handle non-finite values.
Results may differ from a plain program's by a relative error of at most 0.005.
Values may be sent and summed in bfloat16 or wider, within the bound.
A program may use at most 128 MiB of HBM per device.

v0:
```python
import functools

import jax
import jax.numpy as jnp
from jax import lax
from jax.experimental import pallas as pl
from jax.experimental.pallas import tpu as pltpu
from jax.sharding import PartitionSpec as P

GROUPS = 32
EPS = 1e-06
MESH = pl.DeviceIdType.MESH
F32 = jnp.float32
BF16 = jnp.bfloat16


def padded_width(width):
    return (width + 2 + 15) // 16 * 16


def body(
    dims,
    feat_hbm, hid_hbm, cot_hbm, k1_hbm, k2_hbm, gains,
    fgrad, d1, d2, gg,
    feat, hid, cot, k1, k2,
    graw1, graw2, tmp, ext, act, act_t, perm, block_sum,
    acc, acc_in, slope, stats,
    zb_a, xb_a, zb_b, xb_b,
    xs, xa, xb, zf, zs, zr,
    in_sem, halo_s, halo_r, ar_s, ar_r, ch_s, ch_r,
    xa_s, xa_r, xb_s, xb_r, z_s, z_r,
):
    T, H, W, C, half, NT, NS = dims
    WP = padded_width(W)
    per = C // GROUPS
    share = C // (NT * NS)
    R = NT * share
    members = float(T * H * W * per * NT * NS)
    tm, sp, ch = lax.axis_index("tm"), lax.axis_index("space"), lax.axis_index("chan")
    off = pl.multiple_of(ch * half, half)
    wide = 9 * half
    K3 = 3 * half

    def at_z(d):
        return lax.rem(tm + d, NT)

    def at_x(d):
        return lax.rem(sp + d, NS)

    def signal(barrier, where):
        pl.semaphore_signal(barrier, inc=1, device_id=where, device_id_type=MESH)

    def remote(src, dst, s, r, where):
        return pltpu.make_async_remote_copy(
            src_ref=src, dst_ref=dst, send_sem=s, recv_sem=r, device_id=where, device_id_type=MESH
        )

    barrier = pltpu.get_barrier_semaphore()

    @pl.loop(1, NT)
    def _(d):
        signal(barrier, {"tm": at_z(d)})

    for d in range(1, NS):
        signal(barrier, {"space": at_x(d)})
    signal(barrier, {"chan": 1 - ch})
    for dt in (1, NT - 1):
        for ds in (1, NS - 1):
            signal(barrier, {"tm": at_z(dt), "space": at_x(ds)})

    loads = [
        pltpu.make_async_copy(src, dst, in_sem.at[i])
        for i, (src, dst) in enumerate(
            ((feat_hbm, feat), (hid_hbm, hid), (cot_hbm, cot), (k2_hbm, k2), (k1_hbm, k1))
        )
    ]
    for load in loads:
        load.start()

    tmp[...] = jnp.zeros_like(tmp)
    act[...] = jnp.zeros_like(act)
    for graw in (graw2, graw1):
        @pl.when(sp == 0)
        def _():
            graw[:, 0] = jnp.zeros((2 * T, W, half), BF16)

        @pl.when(sp == NS - 1)
        def _():
            graw[:, H + 1] = jnp.zeros((2 * T, W, half), BF16)

        @pl.when(tm == NT - 1)
        def _():
            graw[T : 2 * T] = jnp.zeros((T, H + 2, W, half), BF16)

    rows = lax.broadcasted_iota(jnp.int32, (C, C), 0)
    cols = lax.broadcasted_iota(jnp.int32, (C, C), 1)
    within = lax.rem(rows, R)
    source = within // share * (NS * share) + rows // R * share + lax.rem(within, share)
    perm[...] = jnp.where(cols == source, 1.0, 0.0).astype(BF16)
    block_sum[...] = jnp.where(rows // per == cols // per, 1.0, 0.0).astype(F32)

    def group_sum(values, width):
        return lax.dot_general(
            values, block_sum[0:width, 0:width], (((1,), (0,)), ((), ())),
            precision=lax.Precision.HIGHEST, preferred_element_type=F32,
        )

    def row_of(j):
        return j // H, lax.rem(j, H)

    for load in loads[:3]:
        load.wait()

    def stat_row(j, carry):
        t, h = row_of(j)
        out = []
        for k, ref in enumerate((feat, hid)):
            x = ref[t, h].astype(F32)
            out.append(carry[2 * k] + jnp.sum(x, axis=0, keepdims=True))
            out.append(carry[2 * k + 1] + jnp.sum(x * x, axis=0, keepdims=True))
        graw2[t, h + 1] = cot[t, h, :, pl.ds(off, half)]
        return tuple(out)

    zero_row = jnp.zeros((1, C), F32)
    sums = lax.fori_loop(0, T * H, stat_row, (zero_row,) * 4)
    for k in range(4):
        zb_a[tm, k : k + 1] = sums[k]
    pl.semaphore_wait(barrier, (NT - 1) + (NS - 1) + 1 + 4)

    def along_z(n, zb):
        @pl.loop(1, NT)
        def _(d):
            remote(zb.at[tm], zb.at[tm], ar_s.at[n, 0], ar_r.at[n, 0], {"tm": at_z(d)}).start()

    def z_to_x(n, zb, xbuf):
        every = remote(
            zb.at[0 : NT - 1], zb.at[0 : NT - 1], ar_s.at[n, 0], ar_r.at[n, 0], {"tm": at_z(1)}
        )
        every.wait_recv()
        total = lax.fori_loop(1, NT, lambda j, c: c + zb[j], zb[0])
        xbuf[sp] = total
        for d in range(1, NS):
            remote(xbuf.at[sp], xbuf.at[sp], ar_s.at[n, 1], ar_r.at[n, 1], {"space": at_x(d)}).start()

    def x_total(n, zb, xbuf):
        last = remote(
            xbuf.at[0 : NS - 1], xbuf.at[0 : NS - 1], ar_s.at[n, 1], ar_r.at[n, 1], {"space": at_x(1)}
        )
        last.wait_recv()
        total = xbuf[0]
        for j in range(1, NS):
            total = total + xbuf[j]
        return total

    def reduced_sent(n, zb, xbuf):
        remote(
            zb.at[0 : NT - 1], zb.at[0 : NT - 1], ar_s.at[n, 0], ar_r.at[n, 0], {"tm": at_z(1)}
        ).wait_send()
        remote(
            xbuf.at[0 : NS - 1], xbuf.at[0 : NS - 1], ar_s.at[n, 1], ar_r.at[n, 1], {"space": at_x(1)}
        ).wait_send()

    def halo_copies(n, graw):
        right, left = at_x(1), at_x(NS - 1)
        before = at_z(NT - 1)
        own = pl.ds(0, T)
        later = pl.ds(T, T)
        plan = (
            (graw.at[own, H], graw.at[own, 0], {"space": right}),
            (graw.at[own, 1], graw.at[own, H + 1], {"space": left}),
            (graw.at[own, pl.ds(1, H)], graw.at[later, pl.ds(1, H)], {"tm": before}),
            (graw.at[own, H], graw.at[later, 0], {"tm": before, "space": right}),
            (graw.at[own, 1], graw.at[later, H + 1], {"tm": before, "space": left}),
        )
        return [
            remote(src, dst, halo_s.at[n, i], halo_r.at[n, i], where)
            for i, (src, dst, where) in enumerate(plan)
        ]

    has_right, has_left, has_before, has_after = sp < NS - 1, sp > 0, tm > 0, tm < NT - 1
    sends = (
        has_right,
        has_left,
        has_before,
        jnp.logical_and(has_before, has_right),
        jnp.logical_and(has_before, has_left),
    )
    arrives = (
        has_left,
        has_right,
        has_after,
        jnp.logical_and(has_after, has_left),
        jnp.logical_and(has_after, has_right),
    )

    def halo_start(n, graw):
        for copy, here in zip(halo_copies(n, graw), sends):
            @pl.when(here)
            def _():
                copy.start()

    def halo_wait(n, graw, which):
        copies = halo_copies(n, graw)
        for i in which:
            @pl.when(arrives[i])
            def _():
                copies[i].wait_recv()

    def halo_sent(n, graw):
        for copy, here in zip(halo_copies(n, graw), sends):
            @pl.when(here)
            def _():
                copy.wait_send()

    def shift(graw, first, last):
        @pl.loop(first * (H + 2), last * (H + 2))
        def _(j):
            f, r = j // (H + 2), lax.rem(j, H + 2)
            tmp[8 : 8 + W] = graw[f, r].astype(F32)
            for c in range(3):
                ext[f, r, :, c * half : (c + 1) * half] = tmp[9 - c : 9 - c + WP].astype(BF16)

    def taps(f, a, b):
        return ext[f + 2 - a, 2 - b : 2 - b + H].reshape(H * WP, K3)

    def back_part(kernel, f, a, first):
        left = jnp.concatenate([taps(f, a, b) for b in range(3)], axis=1)
        right = jnp.concatenate([kernel[a * 9 + k] for k in range(9)], axis=1)
        product = lax.dot_general(left, right, (((1,), (1,)), ((), ())), preferred_element_type=F32)
        for k in range(2):
            piece = product[:, k * half : (k + 1) * half].reshape(H, WP, half)
            if first:
                acc[k, f * H : (f + 1) * H] = piece
            else:
                acc[k, f * H : (f + 1) * H] += piece

    def exchange(n):
        return remote(acc.at[1 - ch], acc_in.at[n], ch_s.at[n], ch_r.at[n], {"chan": 1 - ch})

    def delta_part(p, a):
        for b in range(3):
            right = jnp.concatenate([taps(f, a, b) for f in range(T)], axis=0)
            product = lax.dot_general(
                act_t[...], right, (((1,), (0,)), ((), ())), preferred_element_type=F32
            )
            xs[p, :, b * K3 : (b + 1) * K3] = product.astype(BF16)

    def chunk(s, part, parts):
        size = R // parts
        return pl.ds(pl.multiple_of(s * R + part * size, size), size)

    def sum_1(p):
        far = at_x(2)
        return [
            remote(
                xs.at[p, chunk(far, k, 2)], xa.at[p, k], xa_s.at[p, k], xa_r.at[p, k], {"space": at_x(d)}
            )
            for k, d in enumerate((1, NS - 1))
        ]

    def sum_2(p):
        return [
            remote(
                xs.at[p, chunk(at_x(d), 0, 1)], xb.at[p, k], xb_s.at[p, k], xb_r.at[p, k], {"space": at_x(d)}
            )
            for k, d in enumerate((1, NS - 1))
        ]

    def rs_start(p):
        for copy in sum_1(p):
            copy.start()

    def rs_pass(p):
        for k, (first, second) in enumerate(zip(sum_1(p), sum_2(p))):
            first.wait_recv()
            place = chunk(at_x((1, NS - 1)[k]), k, 2)
            xs[p, place] = (xs[p, place].astype(F32) + xa[p, k].astype(F32)).astype(BF16)
            second.start()

    def rs_z(p):
        for copy in sum_2(p):
            copy.wait_recv()
        zf[...] = xs[p, chunk(sp, 0, 1)].astype(F32) + xb[p, 0].astype(F32) + xb[p, 1].astype(F32)
        for t in range(NT):
            zs[p, t] = zf[t * share : (t + 1) * share].astype(BF16)

        @pl.loop(1, NT)
        def _(d):
            remote(zs.at[p, at_z(d)], zr.at[p, d - 1], z_s.at[p], z_r.at[p], {"tm": at_z(d)}).start()

    def z_all(p):
        return remote(zs.at[p, pl.ds(0, NT - 1)], zr.at[p], z_s.at[p], z_r.at[p], {"tm": at_z(1)})

    def rs_end(p, out, a):
        z_all(p).wait_recv()
        total = zs[p, tm].astype(F32)
        total = lax.fori_loop(0, NT - 1, lambda j, c: c + zr[p, j].astype(F32), total)
        for k in range(9):
            out[a * 9 + k] = total[:, k * half : (k + 1) * half]

    def rs_sent(p):
        for copy in sum_1(p) + sum_2(p):
            copy.wait_send()
        z_all(p).wait_send()

    def activate(ref, n):
        @pl.loop(0, T * H)
        def _(j):
            t, h = row_of(j)
            scaled = (ref[t, h].astype(F32) - stats[2 * n : 2 * n + 1]) * stats[2 * n + 1 : 2 * n + 2]
            scaled = scaled * gains[n : n + 1]
            act[j, 0:W] = (scaled * jax.nn.sigmoid(scaled)).astype(BF16)

        act_t[...] = lax.dot_general(
            perm[...], act[...].reshape(T * H * WP, C), (((1,), (1,)), ((), ())),
            preferred_element_type=F32,
        ).astype(BF16)

    def own_row(ref, k):
        return ref[k : k + 1, pl.ds(off, half)]

    def centred_row(ref, n, t, h):
        x = ref[t, h, :, pl.ds(off, half)].astype(F32)
        return (x - own_row(stats, 2 * n)) * own_row(stats, 2 * n + 1)

    def slopes(ref, n):
        exchanged = 1 - n

        def row(j, carry):
            t, h = row_of(j)
            centred = centred_row(ref, n, t, h)
            scaled = centred * own_row(gains, n)
            gate = jax.nn.sigmoid(scaled)
            upstream = acc[ch, j, 0:W] + acc_in[exchanged, j, 0:W]
            value = upstream * gate * (1.0 + scaled * (1.0 - gate))
            slope[j, 0:W] = value
            return (
                carry[0] + jnp.sum(value, axis=0, keepdims=True),
                carry[1] + jnp.sum(value * centred, axis=0, keepdims=True),
            )

        zero = jnp.zeros((1, half), F32)
        return lax.fori_loop(0, T * H, row, (zero, zero))

    def grad_rows(ref, n, totals, store):
        gain = own_row(gains, n)
        both = group_sum(totals * gain, half) * (1.0 / members)
        first, second = both[0:1], both[1:2]
        scale = own_row(stats, 2 * n + 1)
        gg[n : n + 1] = totals[1:2]

        @pl.loop(0, T * H)
        def _(j):
            t, h = row_of(j)
            centred = centred_row(ref, n, t, h)
            store(t, h, scale * (slope[j, 0:W] * gain - first - centred * second))

    def reduce_slopes(n, parts):
        for k in range(2):
            zb_b[n, tm, k : k + 1] = parts[k]
        along_z(2 - n, zb_b.at[n])

    halo_start(0, graw2)
    along_z(0, zb_a)
    z_to_x(0, zb_a, xb_a)
    halo_wait(0, graw2, range(5))
    shift(graw2, 0, 2 * T)
    loads[3].wait()
    for f in range(T):
        for a in (2, 1, 0):
            back_part(k2, f, a, a == 2)
    exchange(0).start()
    totals = group_sum(x_total(0, zb_a, xb_a), C) * (1.0 / members)
    for n in range(2):
        mean = totals[2 * n : 2 * n + 1]
        spread = totals[2 * n + 1 : 2 * n + 2] - mean * mean
        stats[2 * n : 2 * n + 1] = mean
        stats[2 * n + 1 : 2 * n + 2] = lax.rsqrt(spread + EPS)
    exchange(0).wait_recv()
    reduce_slopes(1, slopes(hid, 1))
    activate(hid, 1)
    for p in range(3):
        delta_part(p, 2 - p)
        rs_start(p)
    z_to_x(1, zb_b.at[1], xb_b.at[1])
    rs_pass(0)
    totals_two = x_total(1, zb_b.at[1], xb_b.at[1])

    def store_hidden(t, h, value):
        graw1[t, h + 1] = value.astype(BF16)

    grad_rows(hid, 1, totals_two, store_hidden)

    halo_start(1, graw1)
    rs_pass(1)
    rs_pass(2)
    activate(feat, 0)
    halo_wait(1, graw1, (0, 1))
    shift(graw1, 0, T)
    delta_part(3, 2)
    rs_start(3)
    loads[4].wait()
    exchange(0).wait_send()
    for f in range(T):
        for a in (2, 1):
            if f + 2 - a < T:
                back_part(k1, f, a, a == 2)
    rs_z(0)
    halo_wait(1, graw1, (2, 3, 4))
    shift(graw1, T, 2 * T)
    for f in range(T):
        for a in (1, 0):
            if f + 2 - a >= T:
                back_part(k1, f, a, False)
    exchange(1).start()
    for p in (4, 5):
        delta_part(p, 5 - p)
        rs_start(p)
    exchange(1).wait_recv()
    reduce_slopes(0, slopes(feat, 0))
    rs_pass(3)
    rs_z(1)
    rs_z(2)
    rs_pass(4)
    rs_pass(5)
    z_to_x(2, zb_b.at[0], xb_b.at[0])
    rs_z(3)
    totals_one = x_total(2, zb_b.at[0], xb_b.at[0])

    def store_feature(t, h, value):
        base = cot[t, h, :, pl.ds(off, half)].astype(F32)
        fgrad[t, h] = (base + value).astype(BF16)

    grad_rows(feat, 0, totals_one, store_feature)
    rs_z(4)
    rs_z(5)
    for p in range(6):
        rs_end(p, (d2, d1)[p // 3], 2 - p % 3)

    halo_sent(0, graw2)
    halo_sent(1, graw1)
    reduced_sent(0, zb_a, xb_a)
    reduced_sent(1, zb_b.at[1], xb_b.at[1])
    reduced_sent(2, zb_b.at[0], xb_b.at[0])
    exchange(1).wait_send()
    for p in range(6):
        rs_sent(p)


def shards(features, hidden, cotangent, kernel_one, kernel_two, gains):
    T, H, W, C = features.shape
    half = kernel_one.shape[4]
    NT, NS = lax.axis_size("tm"), lax.axis_size("space")
    share = C // (NT * NS)
    R = NT * share
    WP = padded_width(W)
    wide = 9 * half

    def by_tap(kernel):
        return jnp.transpose(kernel, (1, 2, 3, 0, 4)).reshape(27, C, half)

    vmem = pl.BlockSpec(memory_space=pltpu.VMEM)
    hbm = pl.BlockSpec(memory_space=pl.ANY)
    DMA = pltpu.SemaphoreType.DMA
    call = pl.pallas_call(
        functools.partial(body, (T, H, W, C, half, NT, NS)),
        out_shape=(
            jax.ShapeDtypeStruct((T, H, W, half), BF16),
            jax.ShapeDtypeStruct((27, share, half), F32),
            jax.ShapeDtypeStruct((27, share, half), F32),
            jax.ShapeDtypeStruct((2, half), F32),
        ),
        in_specs=[hbm] * 5 + [vmem],
        out_specs=(vmem,) * 4,
        scratch_shapes=[
            pltpu.VMEM((T, H, W, C), BF16),
            pltpu.VMEM((T, H, W, C), BF16),
            pltpu.VMEM((T, H, W, C), BF16),
            pltpu.VMEM((27, C, half), BF16),
            pltpu.VMEM((27, C, half), BF16),
            pltpu.VMEM((2 * T, H + 2, W, half), BF16),
            pltpu.VMEM((2 * T, H + 2, W, half), BF16),
            pltpu.VMEM((WP + 16, half), F32),
            pltpu.VMEM((2 * T, H + 2, WP, 3 * half), BF16),
            pltpu.VMEM((T * H, WP, C), BF16),
            pltpu.VMEM((C, T * H * WP), BF16),
            pltpu.VMEM((C, C), BF16),
            pltpu.VMEM((C, C), F32),
            pltpu.VMEM((2, T * H, WP, half), F32),
            pltpu.VMEM((2, T * H, WP, half), F32),
            pltpu.VMEM((T * H, WP, half), F32),
            pltpu.VMEM((8, C), F32),
            pltpu.VMEM((NT, 4, C), F32),
            pltpu.VMEM((NS, 4, C), F32),
            pltpu.VMEM((2, NT, 2, half), F32),
            pltpu.VMEM((2, NS, 2, half), F32),
            pltpu.VMEM((6, C, wide), BF16),
            pltpu.VMEM((6, 2, R // 2, wide), BF16),
            pltpu.VMEM((6, 2, R, wide), BF16),
            pltpu.VMEM((R, wide), F32),
            pltpu.VMEM((6, NT, share, wide), BF16),
            pltpu.VMEM((6, NT - 1, share, wide), BF16),
            DMA((5,)),
            DMA((2, 5)),
            DMA((2, 5)),
            DMA((3, 2)),
            DMA((3, 2)),
            DMA((2,)),
            DMA((2,)),
            DMA((6, 2)),
            DMA((6, 2)),
            DMA((6, 2)),
            DMA((6, 2)),
            DMA((6,)),
            DMA((6,)),
        ],
        compiler_params=pltpu.CompilerParams(
            collective_id=0, has_side_effects=True, vmem_limit_bytes=60 * 1024 * 1024
        ),
        name="block_back",
    )
    fgrad, d1, d2, gg = call(
        features, hidden, cotangent, by_tap(kernel_one), by_tap(kernel_two), gains
    )

    def by_channel(delta):
        return jnp.transpose(delta.reshape(3, 3, 3, share, half), (3, 0, 1, 2, 4))

    return (fgrad, by_channel(d1), by_channel(d2), gg)


def solution(mesh):
    placed = (
        P(("clip", "tm"), "space", None, None),
        P(("clip", "tm"), "space", None, None),
        P(("clip", "tm"), "space", None, None),
        P(None, None, None, None, "chan"),
        P(None, None, None, None, "chan"),
        P(),
    )
    return jax.shard_map(
        shards,
        mesh=mesh,
        in_specs=placed,
        out_specs=(
            P(("clip", "tm"), "space", None, "chan"),
            P(("clip", "tm", "space"), None, None, None, "chan"),
            P(("clip", "tm", "space"), None, None, None, "chan"),
            P("clip", "chan"),
        ),
        check_vma=False,
    )
```

profile of v0, /device:TPU:40, one launch (start us, length us, event | category | flops | bytes accessed | tf_op | source)
XLA Modules:
  0.0 116.1 jit_solution(4313601877952025998)
XLA Ops:
  0.6 0.0 copy-start
  0.6 1.8 %copy.10.feat_hbm = bf16[2,4,90,256]{3,2,1,0:T(8,128)(2,1)} copy(bf16[2,4,90,256]{3,1,2,0:T(4,128)(2,1)} %param.6) | data formatting | bytes 737280 | tf_op args[0]
  2.5 1.8 %copy.11.hid_hbm = bf16[2,4,90,256]{3,2,1,0:T(8,128)(2,1)} copy(bf16[2,4,90,256]{3,1,2,0:T(4,128)(2,1)} %param.7) | data formatting | bytes 737280 | tf_op args[1]
  4.2 0.0 copy-done
  4.2 0.8 copy.12.cot_hbm
  5.0 105.3 %block_back.1 = (bf16[2,4,90,128]{3,2,1,0:T(8,128)(2,1)}, f32[27,4,128]{2,1,0:T(4,128)}, f32[27,4,128]{2,1,0:T(4,128)}, f32[2,128]{1,0:T(2,128)}) custom-call(bf16[2,4,90,256]{3,2,1,0:T(8,128)(2,1)} %copy.10.feat_hbm, bf16[2,4,90,256]{3,2,1,0:T(8,128)(2,1)} %copy.11.hid_hbm, bf16[2,4,90,256]{3,2,1,0:T(8,128)(2,1)} %copy.12.cot_hbm, ...), custom_call_target="tpu_custom_call" | custom-call | tf_op jit(solution)/shard_map/block_back/pallas_call | solution.py:522
  110.3 1.7 %copy.13 = bf16[2,4,90,128]{3,1,2,0:T(4,128)(2,1)} copy(bf16[2,4,90,128]{3,2,1,0:T(8,128)(2,1)} %get-tuple-element.12) | data formatting | bytes 368640
  112.0 1.4 %copy.17 = f32[4,3,3,3,128]{4,0,3,2,1:T(4,128)} copy(f32[4,3,3,3,128]{4,0,3,2,1:T(4,128)} %bitcast.15) | data formatting | bytes 110592
  113.5 1.4 %copy.18 = f32[4,3,3,3,128]{4,0,3,2,1:T(4,128)} copy(f32[4,3,3,3,128]{4,0,3,2,1:T(4,128)} %bitcast.14) | data formatting | bytes 110592
  114.9 1.2 %copy.19 = f32[2,128]{1,0:T(2,128)} copy(f32[2,128]{1,0:T(2,128)} %get-tuple-element.23) | data formatting | bytes 2048
Async XLA Ops:
  0.6 3.6 %copy-start = (bf16[2,4,90,256]{3,1,2,0:T(4,128)(2,1)S(1)}, bf16[2,4,90,256]{3,1,2,0:T(4,128)(2,1)}, u32[]{:S(2)}) copy-start(bf16[2,4,90,256]{3,1,2,0:T(4,128)(2,1)} %param.8) | copy-start | bytes 1105924
where the time goes:
time: 117 us; the launch traced here: 116 us
  Pallas kernels  105 us (90%)
  local copies, waits for them, and re-layouts  10.1 us (9%)
    pallas_call x1, Pallas kernels, shards(): call(features, hidden, cotangent, by_tap(kernel_one), by_tap(kernel_two),...  105 us
    unnamed x9, local copies, waits for them, and re-layouts  10.1 us

commit v1 on v0

--- a/solution.py
+++ b/solution.py
@@ -22,13 +22,13 @@
     dims,
     feat_hbm, hid_hbm, cot_hbm, k1_hbm, k2_hbm, gains,
     fgrad, d1, d2, gg,
-    feat, hid, cot, k1, k2,
-    graw1, graw2, tmp, ext, act, act_t, perm, block_sum,
+    feat_n, hid_n, cot_n, feat, hid, k1, k2,
+    graw2, graw1, turn, turn_half, tmp, ext, act, act_t, perm, block_sum, spread_sum,
     acc, acc_in, slope, stats,
     zb_a, xb_a, zb_b, xb_b,
-    xs, xa, xb, zf, zs, zr,
+    xs, xa, xb, zf, zk, zs, za, zc, zr,
     in_sem, halo_s, halo_r, ar_s, ar_r, ch_s, ch_r,
-    xa_s, xa_r, xb_s, xb_r, z_s, z_r,
+    xa_s, xa_r, xb_s, xb_r, za_s, za_r, z_s, z_r,
 ):
     T, H, W, C, half, NT, NS = dims
     WP = padded_width(W)
@@ -71,33 +71,11 @@
     loads = [
         pltpu.make_async_copy(src, dst, in_sem.at[i])
         for i, (src, dst) in enumerate(
-            ((feat_hbm, feat), (hid_hbm, hid), (cot_hbm, cot), (k2_hbm, k2), (k1_hbm, k1))
+            ((feat_hbm, feat_n), (hid_hbm, hid_n), (cot_hbm, cot_n), (k2_hbm, k2), (k1_hbm, k1))
         )
     ]
     for load in loads:
         load.start()
-
-    tmp[...] = jnp.zeros_like(tmp)
-    act[...] = jnp.zeros_like(act)
-    for graw in (graw2, graw1):
-        @pl.when(sp == 0)
-        def _():
-            graw[:, 0] = jnp.zeros((2 * T, W, half), BF16)
-
-        @pl.when(sp == NS - 1)
-        def _():
-            graw[:, H + 1] = jnp.zeros((2 * T, W, half), BF16)
-
-        @pl.when(tm == NT - 1)
-        def _():
-            graw[T : 2 * T] = jnp.zeros((T, H + 2, W, half), BF16)
-
-    rows = lax.broadcasted_iota(jnp.int32, (C, C), 0)
-    cols = lax.broadcasted_iota(jnp.int32, (C, C), 1)
-    within = lax.rem(rows, R)
-    source = within // share * (NS * share) + rows // R * share + lax.rem(within, share)
-    perm[...] = jnp.where(cols == source, 1.0, 0.0).astype(BF16)
-    block_sum[...] = jnp.where(rows // per == cols // per, 1.0, 0.0).astype(F32)
 
     def group_sum(values, width):
         return lax.dot_general(
@@ -111,25 +89,37 @@
     for load in loads[:3]:
         load.wait()
 
-    def stat_row(j, carry):
-        t, h = row_of(j)
+    rows = lax.broadcasted_iota(jnp.int32, (C, half), 0)
+    cols = lax.broadcasted_iota(jnp.int32, (C, half), 1)
+    spread_sum[...] = jnp.where(rows // per == cols, 1.0, 0.0).astype(F32)
+    strip = W // 9 if W % 9 == 0 else 1
+
+    def stat_strip(j, carry):
+        t, w = j // (W // strip), lax.rem(j, W // strip) * strip
         out = []
-        for k, ref in enumerate((feat, hid)):
-            x = ref[t, h].astype(F32)
-            out.append(carry[2 * k] + jnp.sum(x, axis=0, keepdims=True))
-            out.append(carry[2 * k + 1] + jnp.sum(x * x, axis=0, keepdims=True))
-        graw2[t, h + 1] = cot[t, h, :, pl.ds(off, half)]
+        for k, ref in enumerate((feat_n, hid_n)):
+            x = ref[t, pl.ds(w, strip)].astype(F32)
+            out.append(carry[2 * k] + jnp.sum(x, axis=0))
+            out.append(carry[2 * k + 1] + jnp.sum(x * x, axis=0))
         return tuple(out)
 
-    zero_row = jnp.zeros((1, C), F32)
-    sums = lax.fori_loop(0, T * H, stat_row, (zero_row,) * 4)
-    for k in range(4):
-        zb_a[tm, k : k + 1] = sums[k]
+    sums = lax.fori_loop(0, T * (W // strip), stat_strip, (jnp.zeros((H, C), F32),) * 4)
+    sums = jnp.concatenate([jnp.sum(x, axis=0, keepdims=True) for x in sums], axis=0)
+    zb_a[tm] = lax.dot_general(
+        sums, spread_sum[...], (((1,), (0,)), ((), ())),
+        precision=lax.Precision.HIGHEST, preferred_element_type=F32,
+    )
+    for t in range(T):
+        turn_half[t] = cot_n[t, :, :, pl.ds(off, half)].astype(F32)
+        for h in range(H):
+            graw2[t, h + 1] = turn_half[t, :, h, :].astype(BF16)
     pl.semaphore_wait(barrier, (NT - 1) + (NS - 1) + 1 + 4)
 
     def along_z(n, zb):
-        @pl.loop(1, NT)
-        def _(d):
+        @pl.loop(0, NT - 1)
+        def _(k):
+            step = (k + 1) // 2
+            d = NT // 2 + jnp.where(lax.rem(k, 2) == 0, step, -step)
             remote(zb.at[tm], zb.at[tm], ar_s.at[n, 0], ar_r.at[n, 0], {"tm": at_z(d)}).start()
 
     def z_to_x(n, zb, xbuf):
@@ -212,13 +202,16 @@
             def _():
                 copy.wait_send()
 
+    def place_shifted(f, r, values):
+        tmp[8 : 8 + W] = values
+        for c in range(3):
+            ext[f, r, :, c * half : (c + 1) * half] = tmp[9 - c : 9 - c + WP].astype(BF16)
+
     def shift(graw, first, last):
         @pl.loop(first * (H + 2), last * (H + 2))
         def _(j):
             f, r = j // (H + 2), lax.rem(j, H + 2)
-            tmp[8 : 8 + W] = graw[f, r].astype(F32)
-            for c in range(3):
-                ext[f, r, :, c * half : (c + 1) * half] = tmp[9 - c : 9 - c + WP].astype(BF16)
+            place_shifted(f, r, graw[f, r].astype(F32))
 
     def taps(f, a, b):
         return ext[f + 2 - a, 2 - b : 2 - b + H].reshape(H * WP, K3)
@@ -277,30 +270,53 @@
             xs[p, place] = (xs[p, place].astype(F32) + xa[p, k].astype(F32)).astype(BF16)
             second.start()
 
-    def rs_z(p):
+    pairs = NT // 2
+    parity = lax.rem(tm, 2)
+    place = tm // 2
+    mate = tm + 1 - 2 * parity
+
+    def to_mate(p):
+        return remote(zs.at[p, 1 - parity], za.at[p], za_s.at[p], za_r.at[p], {"tm": mate})
+
+    def rs_z1(p):
         for copy in sum_2(p):
             copy.wait_recv()
         zf[...] = xs[p, chunk(sp, 0, 1)].astype(F32) + xb[p, 0].astype(F32) + xb[p, 1].astype(F32)
         for t in range(NT):
-            zs[p, t] = zf[t * share : (t + 1) * share].astype(BF16)
-
-        @pl.loop(1, NT)
+            rows = zf[t * share : (t + 1) * share]
+            zk[p, t % 2, t // 2] = rows
+            zs[p, t % 2, t // 2] = rows.astype(BF16)
+        to_mate(p).start()
+
+    def rs_z2(p):
+        to_mate(p).wait_recv()
+
+        @pl.loop(0, pairs)
+        def _(j):
+            both = zk[p, parity, j] + za[p, j].astype(F32)
+            zk[p, parity, j] = both
+            zc[p, j] = both.astype(BF16)
+
+        @pl.loop(1, pairs)
         def _(d):
-            remote(zs.at[p, at_z(d)], zr.at[p, d - 1], z_s.at[p], z_r.at[p], {"tm": at_z(d)}).start()
+            to = lax.rem(place + d, pairs)
+            remote(zc.at[p, to], zr.at[p, d - 1], z_s.at[p], z_r.at[p], {"tm": 2 * to + parity}).start()
 
     def z_all(p):
-        return remote(zs.at[p, pl.ds(0, NT - 1)], zr.at[p], z_s.at[p], z_r.at[p], {"tm": at_z(1)})
+        return remote(zc.at[p, pl.ds(0, pairs - 1)], zr.at[p], z_s.at[p], z_r.at[p], {"tm": mate})
 
     def rs_end(p, out, a):
         z_all(p).wait_recv()
-        total = zs[p, tm].astype(F32)
-        total = lax.fori_loop(0, NT - 1, lambda j, c: c + zr[p, j].astype(F32), total)
+        total = zk[p, parity, place]
+        for j in range(pairs - 1):
+            total = total + zr[p, j].astype(F32)
         for k in range(9):
             out[a * 9 + k] = total[:, k * half : (k + 1) * half]
 
     def rs_sent(p):
         for copy in sum_1(p) + sum_2(p):
             copy.wait_send()
+        to_mate(p).wait_send()
         z_all(p).wait_send()
 
     def activate(ref, n):
@@ -342,27 +358,72 @@
         zero = jnp.zeros((1, half), F32)
         return lax.fori_loop(0, T * H, row, (zero, zero))
 
-    def grad_rows(ref, n, totals, store):
-        gain = own_row(gains, n)
-        both = group_sum(totals * gain, half) * (1.0 / members)
-        first, second = both[0:1], both[1:2]
-        scale = own_row(stats, 2 * n + 1)
+    def norm_terms(n, totals):
+        both = group_sum(totals * own_row(gains, n), half) * (1.0 / members)
         gg[n : n + 1] = totals[1:2]
+        return both[0:1], both[1:2]
+
+    def grad_row(ref, n, t, h, terms):
+        first, second = terms
+        centred = centred_row(ref, n, t, h)
+        inner = slope[t * H + h, 0:W] * own_row(gains, n) - first - centred * second
+        return own_row(stats, 2 * n + 1) * inner
+
+    def hidden_rows(totals):
+        terms = norm_terms(1, totals)
 
         @pl.loop(0, T * H)
         def _(j):
             t, h = row_of(j)
-            centred = centred_row(ref, n, t, h)
-            store(t, h, scale * (slope[j, 0:W] * gain - first - centred * second))
+            graw1[t, h + 1] = grad_row(hid, 1, t, h, terms).astype(BF16)
+
+    def feature_rows(totals):
+        terms = norm_terms(0, totals)
+
+        @pl.loop(0, T)
+        def _(t):
+            for h in range(H):
+                base = graw2[t, h + 1].astype(F32)
+                turn_half[t, :, h, :] = base + grad_row(feat, 0, t, h, terms)
+            fgrad[t] = turn_half[t].astype(BF16)
+
+    def by_rows(source, target):
+        @pl.loop(0, T)
+        def _(t):
+            turn[...] = source[t].astype(F32)
+            for h in range(H):
+                target[t, h] = turn[:, h, :].astype(BF16)
 
     def reduce_slopes(n, parts):
         for k in range(2):
             zb_b[n, tm, k : k + 1] = parts[k]
         along_z(2 - n, zb_b.at[n])
 
+    along_z(0, zb_a)
     halo_start(0, graw2)
-    along_z(0, zb_a)
-    z_to_x(0, zb_a, xb_a)
+    tmp[...] = jnp.zeros_like(tmp)
+    act[...] = jnp.zeros_like(act)
+    for graw in (graw2, graw1):
+        @pl.when(sp == 0)
+        def _():
+            graw[:, 0] = jnp.zeros((2 * T, W, half), BF16)
+
+        @pl.when(sp == NS - 1)
+        def _():
+            graw[:, H + 1] = jnp.zeros((2 * T, W, half), BF16)
+
+        @pl.when(tm == NT - 1)
+        def _():
+            graw[T : 2 * T] = jnp.zeros((T, H + 2, W, half), BF16)
+
+    rows = lax.broadcasted_iota(jnp.int32, (C, C), 0)
+    cols = lax.broadcasted_iota(jnp.int32, (C, C), 1)
+    within = lax.rem(rows, R)
+    source = within // share * (NS * share) + rows // R * share + lax.rem(within, share)
+    perm[...] = jnp.where(cols == source, 1.0, 0.0).astype(BF16)
+    block_sum[...] = jnp.where(rows // per == cols // per, 1.0, 0.0).astype(F32)
+    by_rows(hid_n, hid)
+    by_rows(feat_n, feat)
     halo_wait(0, graw2, range(5))
     shift(graw2, 0, 2 * T)
     loads[3].wait()
@@ -370,7 +431,11 @@
         for a in (2, 1, 0):
             back_part(k2, f, a, a == 2)
     exchange(0).start()
-    totals = group_sum(x_total(0, zb_a, xb_a), C) * (1.0 / members)
+    z_to_x(0, zb_a, xb_a)
+    totals = lax.dot_general(
+        x_total(0, zb_a, xb_a), spread_sum[...], (((1,), (1,)), ((), ())),
+        precision=lax.Precision.HIGHEST, preferred_element_type=F32,
+    ) * (1.0 / members)
     for n in range(2):
         mean = totals[2 * n : 2 * n + 1]
         spread = totals[2 * n + 1 : 2 * n + 2] - mean * mean
@@ -382,19 +447,15 @@
     for p in range(3):
         delta_part(p, 2 - p)
         rs_start(p)
+    activate(feat, 0)
     z_to_x(1, zb_b.at[1], xb_b.at[1])
     rs_pass(0)
     totals_two = x_total(1, zb_b.at[1], xb_b.at[1])
 
-    def store_hidden(t, h, value):
-        graw1[t, h + 1] = value.astype(BF16)
-
-    grad_rows(hid, 1, totals_two, store_hidden)
-
+    hidden_rows(totals_two)
     halo_start(1, graw1)
     rs_pass(1)
     rs_pass(2)
-    activate(feat, 0)
     halo_wait(1, graw1, (0, 1))
     shift(graw1, 0, T)
     delta_part(3, 2)
@@ -405,35 +466,35 @@
         for a in (2, 1):
             if f + 2 - a < T:
                 back_part(k1, f, a, a == 2)
-    rs_z(0)
+    rs_z1(0)
     halo_wait(1, graw1, (2, 3, 4))
     shift(graw1, T, 2 * T)
+    for p in range(4, 6):
+        delta_part(p, 5 - p)
+        rs_start(p)
+    rs_z1(1)
+    rs_pass(3)
     for f in range(T):
         for a in (1, 0):
             if f + 2 - a >= T:
                 back_part(k1, f, a, False)
     exchange(1).start()
-    for p in (4, 5):
-        delta_part(p, 5 - p)
-        rs_start(p)
+    rs_z1(2)
+    rs_z2(0)
+    rs_pass(4)
     exchange(1).wait_recv()
     reduce_slopes(0, slopes(feat, 0))
-    rs_pass(3)
-    rs_z(1)
-    rs_z(2)
-    rs_pass(4)
     rs_pass(5)
+    rs_z2(1)
+    rs_z2(2)
+    rs_z1(3)
     z_to_x(2, zb_b.at[0], xb_b.at[0])
-    rs_z(3)
-    totals_one = x_total(2, zb_b.at[0], xb_b.at[0])
-
-    def store_feature(t, h, value):
-        base = cot[t, h, :, pl.ds(off, half)].astype(F32)
-        fgrad[t, h] = (base + value).astype(BF16)
-
-    grad_rows(feat, 0, totals_one, store_feature)
-    rs_z(4)
-    rs_z(5)
+    rs_z1(4)
+    rs_z2(3)
+    feature_rows(x_total(2, zb_b.at[0], xb_b.at[0]))
+    rs_z1(5)
+    rs_z2(4)
+    rs_z2(5)
     for p in range(6):
         rs_end(p, (d2, d1)[p // 3], 2 - p % 3)
 
@@ -447,6 +508,12 @@
         rs_sent(p)
 
 
+def hand_on(*refs):
+    count = len(refs) // 2
+    for source, target in zip(refs[:count], refs[count:]):
+        target[...] = source[...]
+
+
 def shards(features, hidden, cotangent, kernel_one, kernel_two, gains):
     T, H, W, C = features.shape
     half = kernel_one.shape[4]
@@ -465,7 +532,7 @@
     call = pl.pallas_call(
         functools.partial(body, (T, H, W, C, half, NT, NS)),
         out_shape=(
-            jax.ShapeDtypeStruct((T, H, W, half), BF16),
+            jax.ShapeDtypeStruct((T, W, H, half), BF16),
             jax.ShapeDtypeStruct((27, share, half), F32),
             jax.ShapeDtypeStruct((27, share, half), F32),
             jax.ShapeDtypeStruct((2, half), F32),
@@ -473,33 +540,41 @@
         in_specs=[hbm] * 5 + [vmem],
         out_specs=(vmem,) * 4,
         scratch_shapes=[
-            pltpu.VMEM((T, H, W, C), BF16),
+            pltpu.VMEM((T, W, H, C), BF16),
+            pltpu.VMEM((T, W, H, C), BF16),
+            pltpu.VMEM((T, W, H, C), BF16),
             pltpu.VMEM((T, H, W, C), BF16),
             pltpu.VMEM((T, H, W, C), BF16),
             pltpu.VMEM((27, C, half), BF16),
             pltpu.VMEM((27, C, half), BF16),
             pltpu.VMEM((2 * T, H + 2, W, half), BF16),
             pltpu.VMEM((2 * T, H + 2, W, half), BF16),
+            pltpu.VMEM((W, H, C), F32),
+            pltpu.VMEM((T, W, H, half), F32),
             pltpu.VMEM((WP + 16, half), F32),
             pltpu.VMEM((2 * T, H + 2, WP, 3 * half), BF16),
             pltpu.VMEM((T * H, WP, C), BF16),
             pltpu.VMEM((C, T * H * WP), BF16),
             pltpu.VMEM((C, C), BF16),
             pltpu.VMEM((C, C), F32),
+            pltpu.VMEM((C, half), F32),
             pltpu.VMEM((2, T * H, WP, half), F32),
             pltpu.VMEM((2, T * H, WP, half), F32),
             pltpu.VMEM((T * H, WP, half), F32),
             pltpu.VMEM((8, C), F32),
-            pltpu.VMEM((NT, 4, C), F32),
-            pltpu.VMEM((NS, 4, C), F32),
+            pltpu.VMEM((NT, 4, half), F32),
+            pltpu.VMEM((NS, 4, half), F32),
             pltpu.VMEM((2, NT, 2, half), F32),
             pltpu.VMEM((2, NS, 2, half), F32),
             pltpu.VMEM((6, C, wide), BF16),
             pltpu.VMEM((6, 2, R // 2, wide), BF16),
             pltpu.VMEM((6, 2, R, wide), BF16),
             pltpu.VMEM((R, wide), F32),
-            pltpu.VMEM((6, NT, share, wide), BF16),
-            pltpu.VMEM((6, NT - 1, share, wide), BF16),
+            pltpu.VMEM((6, 2, NT // 2, share, wide), F32),
+            pltpu.VMEM((6, 2, NT // 2, share, wide), BF16),
+            pltpu.VMEM((6, NT // 2, share, wide), BF16),
+            pltpu.VMEM((6, NT // 2, share, wide), BF16),
+            pltpu.VMEM((6, NT // 2 - 1, share, wide), BF16),
             DMA((5,)),
             DMA((2, 5)),
             DMA((2, 5)),
@@ -513,20 +588,33 @@
             DMA((6, 2)),
             DMA((6,)),
             DMA((6,)),
+            DMA((6,)),
+            DMA((6,)),
         ],
         compiler_params=pltpu.CompilerParams(
             collective_id=0, has_side_effects=True, vmem_limit_bytes=60 * 1024 * 1024
         ),
         name="block_back",
     )
-    fgrad, d1, d2, gg = call(
-        features, hidden, cotangent, by_tap(kernel_one), by_tap(kernel_two), gains
+    def by_column(field):
+        return jnp.transpose(field, (0, 2, 1, 3))
+
+    made = call(
+        by_column(features), by_column(hidden), by_column(cotangent),
+        by_tap(kernel_one), by_tap(kernel_two), gains,
     )
+    fgrad, d1, d2, gg = pl.pallas_call(
+        hand_on,
+        out_shape=tuple(jax.ShapeDtypeStruct(x.shape, x.dtype) for x in made),
+        in_specs=[vmem] * 4,
+        out_specs=(vmem,) * 4,
+        name="hand_on",
+    )(*made)
 
     def by_channel(delta):
         return jnp.transpose(delta.reshape(3, 3, 3, share, half), (3, 0, 1, 2, 4))
 
-    return (fgrad, by_channel(d1), by_channel(d2), gg)
+    return (by_column(fgrad), by_channel(d1), by_channel(d2), gg)
 
 
 def solution(mesh):

time: 117 us -> 101 us (0.86); the launches traced: 116 us -> 101 us
  local copies, waits for them, and re-layouts: 10.1 us -> 0 us
  Pallas kernels: 105 us -> 101 us
    unnamed x9 -> x0, local copies, waits for them, and re-layouts: 10.1 us -> none
    pallas_call x1 -> x2, Pallas kernels: 105 us -> 101 us  [the longest x1 99 us: shards(): call(by_column(features), by_column(hidden), by_column(cotangent), by_tap...]
where the time goes in v1:
time: 101 us
  Pallas kernels  101 us (100%)
    pallas_call x1, Pallas kernels, shards(): call(by_column(features), by_column(hidden), by_column(cotangent), by_tap...  99 us

profile of v1, /device:TPU:40, one launch (start us, length us, event | category | flops | bytes accessed | tf_op | source)
XLA Modules:
  0.0 101.3 jit_solution(2398313239701982502)
XLA Ops:
  0.6 99.0 %block_back.1 = (bf16[2,90,4,128]{3,2,1,0:T(4,128)(2,1)}, f32[27,4,128]{2,1,0:T(4,128)}, f32[27,4,128]{2,1,0:T(4,128)}, f32[2,128]{1,0:T(2,128)}) custom-call(bf16[2,90,4,256]{3,2,1,0:T(4,128)(2,1)} %bitcast.18, bf16[2,90,4,256]{3,2,1,0:T(4,128)(2,1)} %bitcast.19, bf16[2,90,4,256]{3,2,1,0:T(4,128)(2,1)} %bitcast.20, bf16[27,256,128]{2,1,0:T(8,128)(2,1)} %bitcast.16, ...), custom_call_target="tpu_custom_call" | custom-call | tf_op jit(solution)/shard_map/block_back/pallas_call | solution.py:602
  99.6 1.7 %hand_on.1 = (bf16[2,90,4,128]{3,2,1,0:T(4,128)(2,1)}, f32[27,4,128]{2,1,0:T(4,128)}, f32[27,4,128]{2,1,0:T(4,128)}, f32[2,128]{1,0:T(2,128)}) custom-call(bf16[2,90,4,128]{3,2,1,0:T(4,128)(2,1)} %get-tuple-element.12.refs_0_, f32[27,4,128]{2,1,0:T(4,128)} %get-tuple-element.13.refs_1_, f32[27,4,128]{2,1,0:T(4,128)} %get-tuple-element.14.refs_2_, ...), custom_call_target="tpu_custom_call" | custom-call | tf_op jit(solution)/shard_map/hand_on/pallas_call | solution.py:606

commit v2 on v1

--- a/solution.py
+++ b/solution.py
@@ -8,6 +8,7 @@
 from jax.sharding import PartitionSpec as P
 
 GROUPS = 32
+PIECES = ((0, 0, 3), (1, 0, 3), (2, 0, 3), (3, 0, 3), (4, 0, 3), (5, 0, 1), (5, 1, 2), (5, 2, 3))
 EPS = 1e-06
 MESH = pl.DeviceIdType.MESH
 F32 = jnp.float32
@@ -26,9 +27,9 @@
     graw2, graw1, turn, turn_half, tmp, ext, act, act_t, perm, block_sum, spread_sum,
     acc, acc_in, slope, stats,
     zb_a, xb_a, zb_b, xb_b,
-    xs, xa, xb, zf, zk, zs, za, zc, zr,
+    xs, xa, xb, zf, zk, zs, za, zc, zr, ring, ring_k, ring_s, ring_r,
     in_sem, halo_s, halo_r, ar_s, ar_r, ch_s, ch_r,
-    xa_s, xa_r, xb_s, xb_r, za_s, za_r, z_s, z_r,
+    xa_s, xa_r, xb_s, xb_r, za_s, za_r, z_s, z_r, hop_s, hop_r, last_s, last_r,
 ):
     T, H, W, C, half, NT, NS = dims
     WP = padded_width(W)
@@ -55,6 +56,15 @@
             src_ref=src, dst_ref=dst, send_sem=s, recv_sem=r, device_id=where, device_id_type=MESH
         )
 
+    loads = [
+        pltpu.make_async_copy(src, dst, in_sem.at[i])
+        for i, (src, dst) in enumerate(
+            ((feat_hbm, feat_n), (hid_hbm, hid_n), (cot_hbm, cot_n), (k2_hbm, k2), (k1_hbm, k1))
+        )
+    ]
+    for load in loads:
+        load.start()
+
     barrier = pltpu.get_barrier_semaphore()
 
     @pl.loop(1, NT)
@@ -67,15 +77,6 @@
     for dt in (1, NT - 1):
         for ds in (1, NS - 1):
             signal(barrier, {"tm": at_z(dt), "space": at_x(ds)})
-
-    loads = [
-        pltpu.make_async_copy(src, dst, in_sem.at[i])
-        for i, (src, dst) in enumerate(
-            ((feat_hbm, feat_n), (hid_hbm, hid_n), (cot_hbm, cot_n), (k2_hbm, k2), (k1_hbm, k1))
-        )
-    ]
-    for load in loads:
-        load.start()
 
     def group_sum(values, width):
         return lax.dot_general(
@@ -230,13 +231,19 @@
     def exchange(n):
         return remote(acc.at[1 - ch], acc_in.at[n], ch_s.at[n], ch_r.at[n], {"chan": 1 - ch})
 
-    def delta_part(p, a):
-        for b in range(3):
+    def lanes(p):
+        q, low, high = PIECES[p]
+        return q, pl.ds(low * K3, (high - low) * K3)
+
+    def delta_part(p):
+        q, low, high = PIECES[p]
+        a = 2 - q % 3
+        for b in range(low, high):
             right = jnp.concatenate([taps(f, a, b) for f in range(T)], axis=0)
             product = lax.dot_general(
                 act_t[...], right, (((1,), (0,)), ((), ())), preferred_element_type=F32
             )
-            xs[p, :, b * K3 : (b + 1) * K3] = product.astype(BF16)
+            xs[q, :, b * K3 : (b + 1) * K3] = product.astype(BF16)
 
     def chunk(s, part, parts):
         size = R // parts
@@ -244,17 +251,21 @@
 
     def sum_1(p):
         far = at_x(2)
+        q, cut = lanes(p)
         return [
             remote(
-                xs.at[p, chunk(far, k, 2)], xa.at[p, k], xa_s.at[p, k], xa_r.at[p, k], {"space": at_x(d)}
+                xs.at[q, chunk(far, k, 2), cut], xa.at[q, k, :, cut],
+                xa_s.at[p, k], xa_r.at[p, k], {"space": at_x(d)},
             )
             for k, d in enumerate((1, NS - 1))
         ]
 
     def sum_2(p):
+        q, cut = lanes(p)
         return [
             remote(
-                xs.at[p, chunk(at_x(d), 0, 1)], xb.at[p, k], xb_s.at[p, k], xb_r.at[p, k], {"space": at_x(d)}
+                xs.at[q, chunk(at_x(d), 0, 1), cut], xb.at[q, k, :, cut],
+                xb_s.at[p, k], xb_r.at[p, k], {"space": at_x(d)},
             )
             for k, d in enumerate((1, NS - 1))
         ]
@@ -264,54 +275,74 @@
             copy.start()
 
     def rs_pass(p):
+        q, cut = lanes(p)
         for k, (first, second) in enumerate(zip(sum_1(p), sum_2(p))):
             first.wait_recv()
-            place = chunk(at_x((1, NS - 1)[k]), k, 2)
-            xs[p, place] = (xs[p, place].astype(F32) + xa[p, k].astype(F32)).astype(BF16)
+            rows = chunk(at_x((1, NS - 1)[k]), k, 2)
+            xs[q, rows, cut] = (xs[q, rows, cut].astype(F32) + xa[q, k, :, cut].astype(F32)).astype(BF16)
             second.start()
 
     pairs = NT // 2
     parity = lax.rem(tm, 2)
     place = tm // 2
-    mate = tm + 1 - 2 * parity
+
+    def mate(p):
+        turned = parity if p % 2 == 0 else 1 - parity
+        return {"tm": lax.rem(tm + 1 - 2 * turned + NT, NT)}
 
     def to_mate(p):
-        return remote(zs.at[p, 1 - parity], za.at[p], za_s.at[p], za_r.at[p], {"tm": mate})
+        q, cut = lanes(p)
+        return remote(
+            zs.at[q, 1 - parity, :, :, cut], za.at[q, :, :, cut], za_s.at[p], za_r.at[p], mate(p)
+        )
 
     def rs_z1(p):
+        q, cut = lanes(p)
         for copy in sum_2(p):
             copy.wait_recv()
-        zf[...] = xs[p, chunk(sp, 0, 1)].astype(F32) + xb[p, 0].astype(F32) + xb[p, 1].astype(F32)
+        kept = xs[q, chunk(sp, 0, 1), cut].astype(F32)
+        zf[:, cut] = kept + xb[q, 0, :, cut].astype(F32) + xb[q, 1, :, cut].astype(F32)
         for t in range(NT):
-            rows = zf[t * share : (t + 1) * share]
-            zk[p, t % 2, t // 2] = rows
-            zs[p, t % 2, t // 2] = rows.astype(BF16)
+            rows = zf[t * share : (t + 1) * share, cut]
+            zk[q, t % 2, t // 2, :, cut] = rows
+            zs[q, t % 2, t // 2, :, cut] = rows.astype(BF16)
         to_mate(p).start()
 
     def rs_z2(p):
+        q, cut = lanes(p)
         to_mate(p).wait_recv()
 
         @pl.loop(0, pairs)
         def _(j):
-            both = zk[p, parity, j] + za[p, j].astype(F32)
-            zk[p, parity, j] = both
-            zc[p, j] = both.astype(BF16)
+            both = zk[q, parity, j, :, cut] + za[q, j, :, cut].astype(F32)
+            zk[q, parity, j, :, cut] = both
+            zc[q, j, :, cut] = both.astype(BF16)
 
         @pl.loop(1, pairs)
-        def _(d):
+        def _(k):
+            d = lax.rem(k + pairs // 2 - 1, pairs - 1) + 1
             to = lax.rem(place + d, pairs)
-            remote(zc.at[p, to], zr.at[p, d - 1], z_s.at[p], z_r.at[p], {"tm": 2 * to + parity}).start()
+            remote(
+                zc.at[q, to, :, cut], zr.at[q, d - 1, :, cut], z_s.at[p], z_r.at[p],
+                {"tm": 2 * to + parity},
+            ).start()
 
     def z_all(p):
-        return remote(zc.at[p, pl.ds(0, pairs - 1)], zr.at[p], z_s.at[p], z_r.at[p], {"tm": mate})
-
-    def rs_end(p, out, a):
+        q, cut = lanes(p)
+        return remote(
+            zc.at[q, pl.ds(0, pairs - 1), :, cut], zr.at[q, :, :, cut], z_s.at[p], z_r.at[p], mate(p)
+        )
+
+    def rs_end(p):
+        q, low, high = PIECES[p]
+        cut = lanes(p)[1]
         z_all(p).wait_recv()
-        total = zk[p, parity, place]
+        total = zk[q, parity, place, :, cut]
         for j in range(pairs - 1):
-            total = total + zr[p, j].astype(F32)
-        for k in range(9):
-            out[a * 9 + k] = total[:, k * half : (k + 1) * half]
+            total = total + zr[q, j, :, cut].astype(F32)
+        out, a = (d2, d1)[q // 3], 2 - q % 3
+        for k in range(3 * (high - low)):
+            out[a * 9 + 3 * low + k] = total[:, k * half : (k + 1) * half]
 
     def rs_sent(p):
         for copy in sum_1(p) + sum_2(p):
@@ -319,7 +350,71 @@
         to_mate(p).wait_send()
         z_all(p).wait_send()
 
-    def activate(ref, n):
+    deep = NT // 2
+    band = NS * share
+
+    def band_of(t):
+        return pl.ds(pl.multiple_of(t * band, band), band)
+
+    def hop(q, way, k):
+        if way == 0:
+            dest, to, slot = at_z(deep - k), at_z(1), k
+        else:
+            dest, to, slot = at_z(NT - deep + 1 + k), at_z(NT - 1), deep + k
+        return dest, remote(
+            xs.at[q, band_of(dest)], ring.at[q, slot], hop_s.at[q, slot], hop_r.at[q, slot], {"tm": to}
+        )
+
+    def tick(q, k):
+        for way in range(2):
+            if k >= deep - way:
+                continue
+            dest, copy = hop(q, way, k)
+            if k > 0:
+                hop(q, way, k - 1)[1].wait_recv()
+                came = ring[q, way * deep + k - 1].astype(F32)
+                xs[q, band_of(dest)] = (xs[q, band_of(dest)].astype(F32) + came).astype(BF16)
+            copy.start()
+
+    def ticks(k):
+        for q in range(3):
+            tick(q, k)
+
+    def across(q, d):
+        return remote(
+            ring_s.at[q, at_x(d)], ring_r.at[q, d - 1], last_s.at[q, d - 1], last_r.at[q, d - 1],
+            {"space": at_x(d)},
+        )
+
+    def ring_pass(q):
+        for way in range(2):
+            hop(q, way, deep - 1 - way)[1].wait_recv()
+        total = xs[q, band_of(tm)].astype(F32)
+        total = total + ring[q, deep - 1].astype(F32) + ring[q, 2 * deep - 2].astype(F32)
+        zf[0:band] = total
+        for x in range(NS):
+            rows = zf[x * share : (x + 1) * share]
+            ring_k[q, x] = rows
+            ring_s[q, x] = rows.astype(BF16)
+        for d in range(1, NS):
+            across(q, d).start()
+
+    def ring_end(q):
+        total = ring_k[q, sp]
+        for d in range(1, NS):
+            across(q, d).wait_recv()
+            total = total + ring_r[q, d - 1].astype(F32)
+        for k in range(9):
+            d2[(2 - q) * 9 + k] = total[:, k * half : (k + 1) * half]
+
+    def ring_sent(q):
+        for way in range(2):
+            for k in range(deep - way):
+                hop(q, way, k)[1].wait_send()
+        for d in range(1, NS):
+            across(q, d).wait_send()
+
+    def activate(ref, n, order):
         @pl.loop(0, T * H)
         def _(j):
             t, h = row_of(j)
@@ -328,7 +423,7 @@
             act[j, 0:W] = (scaled * jax.nn.sigmoid(scaled)).astype(BF16)
 
         act_t[...] = lax.dot_general(
-            perm[...], act[...].reshape(T * H * WP, C), (((1,), (1,)), ((), ())),
+            order, act[...].reshape(T * H * WP, C), (((1,), (1,)), ((), ())),
             preferred_element_type=F32,
         ).astype(BF16)
 
@@ -421,17 +516,26 @@
     within = lax.rem(rows, R)
     source = within // share * (NS * share) + rows // R * share + lax.rem(within, share)
     perm[...] = jnp.where(cols == source, 1.0, 0.0).astype(BF16)
+    same = rows == cols
     block_sum[...] = jnp.where(rows // per == cols // per, 1.0, 0.0).astype(F32)
     by_rows(hid_n, hid)
     by_rows(feat_n, feat)
-    halo_wait(0, graw2, range(5))
-    shift(graw2, 0, 2 * T)
+
+    def back_parts(kernel, later):
+        for f in range(T):
+            for a in (2, 1, 0):
+                if (f + 2 - a >= T) == later:
+                    back_part(kernel, f, a, a == 2)
+
+    halo_wait(0, graw2, (0, 1))
+    shift(graw2, 0, T)
     loads[3].wait()
-    for f in range(T):
-        for a in (2, 1, 0):
-            back_part(k2, f, a, a == 2)
+    back_parts(k2, False)
+    z_to_x(0, zb_a, xb_a)
+    halo_wait(0, graw2, (2, 3, 4))
+    shift(graw2, T, 2 * T)
+    back_parts(k2, True)
     exchange(0).start()
-    z_to_x(0, zb_a, xb_a)
     totals = lax.dot_general(
         x_total(0, zb_a, xb_a), spread_sum[...], (((1,), (1,)), ((), ())),
         precision=lax.Precision.HIGHEST, preferred_element_type=F32,
@@ -443,60 +547,59 @@
         stats[2 * n + 1 : 2 * n + 2] = lax.rsqrt(spread + EPS)
     exchange(0).wait_recv()
     reduce_slopes(1, slopes(hid, 1))
-    activate(hid, 1)
+    activate(hid, 1, jnp.where(same, 1.0, 0.0).astype(BF16))
     for p in range(3):
-        delta_part(p, 2 - p)
-        rs_start(p)
-    activate(feat, 0)
+        delta_part(p)
+        tick(p, 0)
+    activate(feat, 0, perm[...])
     z_to_x(1, zb_b.at[1], xb_b.at[1])
-    rs_pass(0)
+    ticks(1)
     totals_two = x_total(1, zb_b.at[1], xb_b.at[1])
 
     hidden_rows(totals_two)
     halo_start(1, graw1)
-    rs_pass(1)
-    rs_pass(2)
+    ticks(2)
     halo_wait(1, graw1, (0, 1))
     shift(graw1, 0, T)
-    delta_part(3, 2)
+    delta_part(3)
     rs_start(3)
     loads[4].wait()
     exchange(0).wait_send()
-    for f in range(T):
-        for a in (2, 1):
-            if f + 2 - a < T:
-                back_part(k1, f, a, a == 2)
-    rs_z1(0)
+    back_parts(k1, False)
+    ticks(3)
     halo_wait(1, graw1, (2, 3, 4))
     shift(graw1, T, 2 * T)
-    for p in range(4, 6):
-        delta_part(p, 5 - p)
+    for p in range(4, 8):
+        delta_part(p)
         rs_start(p)
-    rs_z1(1)
     rs_pass(3)
-    for f in range(T):
-        for a in (1, 0):
-            if f + 2 - a >= T:
-                back_part(k1, f, a, False)
+    ticks(4)
+    back_parts(k1, True)
     exchange(1).start()
-    rs_z1(2)
-    rs_z2(0)
     rs_pass(4)
+    for p in range(5, 8):
+        rs_pass(p)
+    ticks(5)
     exchange(1).wait_recv()
     reduce_slopes(0, slopes(feat, 0))
-    rs_pass(5)
-    rs_z2(1)
-    rs_z2(2)
     rs_z1(3)
+    ticks(6)
+    rs_z1(4)
+    for p in range(5, 8):
+        rs_z1(p)
+    ticks(7)
+    rs_z2(3)
+    rs_z2(4)
     z_to_x(2, zb_b.at[0], xb_b.at[0])
-    rs_z1(4)
-    rs_z2(3)
+    for p in range(5, 8):
+        rs_z2(p)
+    for q in range(3):
+        ring_pass(q)
     feature_rows(x_total(2, zb_b.at[0], xb_b.at[0]))
-    rs_z1(5)
-    rs_z2(4)
-    rs_z2(5)
-    for p in range(6):
-        rs_end(p, (d2, d1)[p // 3], 2 - p % 3)
+    for q in range(3):
+        ring_end(q)
+    for p in range(3, 8):
+        rs_end(p)
 
     halo_sent(0, graw2)
     halo_sent(1, graw1)
@@ -504,8 +607,10 @@
     reduced_sent(1, zb_b.at[1], xb_b.at[1])
     reduced_sent(2, zb_b.at[0], xb_b.at[0])
     exchange(1).wait_send()
-    for p in range(6):
+    for p in range(3, 8):
         rs_sent(p)
+    for q in range(3):
+        ring_sent(q)
 
 
 def hand_on(*refs):
@@ -575,6 +680,10 @@
             pltpu.VMEM((6, NT // 2, share, wide), BF16),
             pltpu.VMEM((6, NT // 2, share, wide), BF16),
             pltpu.VMEM((6, NT // 2 - 1, share, wide), BF16),
+            pltpu.VMEM((3, NT - 1, NS * share, wide), BF16),
+            pltpu.VMEM((3, NS, share, wide), F32),
+            pltpu.VMEM((3, NS, share, wide), BF16),
+            pltpu.VMEM((3, NS - 1, share, wide), BF16),
             DMA((5,)),
             DMA((2, 5)),
             DMA((2, 5)),
@@ -582,14 +691,18 @@
             DMA((3, 2)),
             DMA((2,)),
             DMA((2,)),
-            DMA((6, 2)),
-            DMA((6, 2)),
-            DMA((6, 2)),
-            DMA((6, 2)),
-            DMA((6,)),
-            DMA((6,)),
-            DMA((6,)),
-            DMA((6,)),
+            DMA((8, 2)),
+            DMA((8, 2)),
+            DMA((8, 2)),
+            DMA((8, 2)),
+            DMA((8,)),
+            DMA((8,)),
+            DMA((8,)),
+            DMA((8,)),
+            DMA((3, NT - 1)),
+            DMA((3, NT - 1)),
+            DMA((3, NS - 1)),
+            DMA((3, NS - 1)),
         ],
         compiler_params=pltpu.CompilerParams(
             collective_id=0, has_side_effects=True, vmem_limit_bytes=60 * 1024 * 1024

time: 101 us -> 97.8 us (0.968)
  Pallas kernels: 101 us -> 97 us
    pallas_call x1, Pallas kernels: 99 us -> 95.3 us  [shards(): call(by_column(features), by_column(hidden), by_column(cotangent), by_tap...]
where the time goes in v2:
time: 97.8 us; the launch traced here: 97.6 us
  Pallas kernels  97 us (99%)
    pallas_call x1, Pallas kernels, shards(): call(by_column(features), by_column(hidden), by_column(cotangent), by_tap...  95.3 us

profile of v2, /device:TPU:40, one launch (start us, length us, event | category | flops | bytes accessed | tf_op | source)
XLA Modules:
  0.0 97.6 jit_solution(1327795476781542023)
XLA Ops:
  0.6 95.3 %block_back.1 = (bf16[2,90,4,128]{3,2,1,0:T(4,128)(2,1)}, f32[27,4,128]{2,1,0:T(4,128)}, f32[27,4,128]{2,1,0:T(4,128)}, f32[2,128]{1,0:T(2,128)}) custom-call(bf16[2,90,4,256]{3,2,1,0:T(4,128)(2,1)} %bitcast.18, bf16[2,90,4,256]{3,2,1,0:T(4,128)(2,1)} %bitcast.19, bf16[2,90,4,256]{3,2,1,0:T(4,128)(2,1)} %bitcast.20, bf16[27,256,128]{2,1,0:T(8,128)(2,1)} %bitcast.16, ...), custom_call_target="tpu_custom_call" | custom-call | tf_op jit(solution)/shard_map/block_back/pallas_call | solution.py:715
  96.0 1.7 %hand_on.1 = (bf16[2,90,4,128]{3,2,1,0:T(4,128)(2,1)}, f32[27,4,128]{2,1,0:T(4,128)}, f32[27,4,128]{2,1,0:T(4,128)}, f32[2,128]{1,0:T(2,128)}) custom-call(bf16[2,90,4,128]{3,2,1,0:T(4,128)(2,1)} %get-tuple-element.12.refs_0_, f32[27,4,128]{2,1,0:T(4,128)} %get-tuple-element.13.refs_1_, f32[27,4,128]{2,1,0:T(4,128)} %get-tuple-element.14.refs_2_, ...), custom_call_target="tpu_custom_call" | custom-call | tf_op jit(solution)/shard_map/hand_on/pallas_call | solution.py:719

commit v3 on v2

--- a/solution.py
+++ b/solution.py
@@ -23,8 +23,8 @@
     dims,
     feat_hbm, hid_hbm, cot_hbm, k1_hbm, k2_hbm, gains,
     fgrad, d1, d2, gg,
-    feat_n, hid_n, cot_n, feat, hid, k1, k2,
-    graw2, graw1, turn, turn_half, tmp, ext, act, act_t, perm, block_sum, spread_sum,
+    feat_n, hid_n, cot_n, wide_feat, hid, k1, k2,
+    graw2, graw1, turn, turn_half, tmp, ext, act, act_t, wide_act, wide_act_t, own_f, perm, block_sum, spread_sum,
     acc, acc_in, slope, stats,
     zb_a, xb_a, zb_b, xb_b,
     xs, xa, xb, zf, zk, zs, za, zc, zr, ring, ring_k, ring_s, ring_r,
@@ -41,6 +41,7 @@
     off = pl.multiple_of(ch * half, half)
     wide = 9 * half
     K3 = 3 * half
+    feat = wide_feat.at[pl.ds(T, T), pl.ds(1, H)]
 
     def at_z(d):
         return lax.rem(tm + d, NT)
@@ -203,6 +204,55 @@
             def _():
                 copy.wait_send()
 
+    def feature_copies():
+        right, left, after = at_x(1), at_x(NS - 1), at_z(1)
+        own, earlier = pl.ds(T, T), pl.ds(0, T)
+        w = wide_feat
+        plan = (
+            (w.at[own, H], w.at[own, 0], {"space": right}),
+            (w.at[own, 1], w.at[own, H + 1], {"space": left}),
+            (w.at[own, pl.ds(1, H)], w.at[earlier, pl.ds(1, H)], {"tm": after}),
+            (w.at[own, H], w.at[earlier, 0], {"tm": after, "space": right}),
+            (w.at[own, 1], w.at[earlier, H + 1], {"tm": after, "space": left}),
+        )
+        return [
+            remote(src, dst, halo_s.at[2, i], halo_r.at[2, i], where)
+            for i, (src, dst, where) in enumerate(plan)
+        ]
+
+    feature_sends = (
+        has_right,
+        has_left,
+        has_after,
+        jnp.logical_and(has_after, has_right),
+        jnp.logical_and(has_after, has_left),
+    )
+    feature_arrives = (
+        has_left,
+        has_right,
+        has_before,
+        jnp.logical_and(has_before, has_left),
+        jnp.logical_and(has_before, has_right),
+    )
+
+    def feature_start():
+        for copy, here in zip(feature_copies(), feature_sends):
+            @pl.when(here)
+            def _():
+                copy.start()
+
+    def feature_wait():
+        for copy, here in zip(feature_copies(), feature_arrives):
+            @pl.when(here)
+            def _():
+                copy.wait_recv()
+
+    def feature_sent():
+        for copy, here in zip(feature_copies(), feature_sends):
+            @pl.when(here)
+            def _():
+                copy.wait_send()
+
     def place_shifted(f, r, values):
         tmp[8 : 8 + W] = values
         for c in range(3):
@@ -212,6 +262,17 @@
         @pl.loop(first * (H + 2), last * (H + 2))
         def _(j):
             f, r = j // (H + 2), lax.rem(j, H + 2)
+            place_shifted(f, r, graw[f, r].astype(F32))
+
+    def shift_own(graw):
+        @pl.loop(0, T * H)
+        def _(j):
+            place_shifted(j // H, lax.rem(j, H) + 1, graw[j // H, lax.rem(j, H) + 1].astype(F32))
+
+    def shift_edges(graw):
+        @pl.loop(0, 2 * T)
+        def _(j):
+            f, r = j // 2, lax.rem(j, 2) * (H + 1)
             place_shifted(f, r, graw[f, r].astype(F32))
 
     def taps(f, a, b):
@@ -239,11 +300,18 @@
         q, low, high = PIECES[p]
         a = 2 - q % 3
         for b in range(low, high):
-            right = jnp.concatenate([taps(f, a, b) for f in range(T)], axis=0)
+            if q < 3:
+                left = act_t[...]
+                right = jnp.concatenate([taps(f, a, b) for f in range(T)], axis=0)
+            else:
+                left = wide_act_t[b, :, a * H * WP : (a + T) * H * WP]
+                right = jnp.concatenate([taps(f, 2, 1) for f in range(T)], axis=0)
             product = lax.dot_general(
-                act_t[...], right, (((1,), (0,)), ((), ())), preferred_element_type=F32
+                left, right, (((1,), (0,)), ((), ())), preferred_element_type=F32
             )
             xs[q, :, b * K3 : (b + 1) * K3] = product.astype(BF16)
+            if q < 3:
+                own_f[q, :, b * K3 : (b + 1) * K3] = product
 
     def chunk(s, part, parts):
         size = R // parts
@@ -350,7 +418,7 @@
         to_mate(p).wait_send()
         z_all(p).wait_send()
 
-    deep = NT // 2
+    steps = (NT // 2, NT - 1 - NT // 2)
     band = NS * share
 
     def band_of(t):
@@ -358,27 +426,24 @@
 
     def hop(q, way, k):
         if way == 0:
-            dest, to, slot = at_z(deep - k), at_z(1), k
+            dest, to, slot = at_z(steps[0] - k), at_z(1), k
         else:
-            dest, to, slot = at_z(NT - deep + 1 + k), at_z(NT - 1), deep + k
+            dest, to, slot = at_z(NT - steps[1] + k), at_z(NT - 1), steps[0] + k
         return dest, remote(
             xs.at[q, band_of(dest)], ring.at[q, slot], hop_s.at[q, slot], hop_r.at[q, slot], {"tm": to}
         )
 
-    def tick(q, k):
-        for way in range(2):
-            if k >= deep - way:
-                continue
-            dest, copy = hop(q, way, k)
-            if k > 0:
-                hop(q, way, k - 1)[1].wait_recv()
-                came = ring[q, way * deep + k - 1].astype(F32)
-                xs[q, band_of(dest)] = (xs[q, band_of(dest)].astype(F32) + came).astype(BF16)
-            copy.start()
-
-    def ticks(k):
+    def tick(q, way, k):
+        dest, copy = hop(q, way, k)
+        if k > 0:
+            hop(q, way, k - 1)[1].wait_recv()
+            came = ring[q, way * steps[0] + k - 1].astype(F32)
+            xs[q, band_of(dest)] = (own_f[q, band_of(dest)] + came).astype(BF16)
+        copy.start()
+
+    def ticks(way, k):
         for q in range(3):
-            tick(q, k)
+            tick(q, way, k)
 
     def across(q, d):
         return remote(
@@ -388,9 +453,9 @@
 
     def ring_pass(q):
         for way in range(2):
-            hop(q, way, deep - 1 - way)[1].wait_recv()
-        total = xs[q, band_of(tm)].astype(F32)
-        total = total + ring[q, deep - 1].astype(F32) + ring[q, 2 * deep - 2].astype(F32)
+            hop(q, way, steps[way] - 1)[1].wait_recv()
+        total = own_f[q, band_of(tm)]
+        total = total + ring[q, steps[0] - 1].astype(F32) + ring[q, NT - 2].astype(F32)
         zf[0:band] = total
         for x in range(NS):
             rows = zf[x * share : (x + 1) * share]
@@ -409,23 +474,44 @@
 
     def ring_sent(q):
         for way in range(2):
-            for k in range(deep - way):
+            for k in range(steps[way]):
                 hop(q, way, k)[1].wait_send()
         for d in range(1, NS):
             across(q, d).wait_send()
 
-    def activate(ref, n, order):
+    def activated(x, n):
+        scaled = (x.astype(F32) - stats[2 * n : 2 * n + 1]) * stats[2 * n + 1 : 2 * n + 2]
+        scaled = scaled * gains[n : n + 1]
+        return scaled * jax.nn.sigmoid(scaled)
+
+    def turned(order, cells):
+        return lax.dot_general(
+            order, cells, (((1,), (1,)), ((), ())), preferred_element_type=F32
+        ).astype(BF16)
+
+    def activate_hidden():
         @pl.loop(0, T * H)
         def _(j):
             t, h = row_of(j)
-            scaled = (ref[t, h].astype(F32) - stats[2 * n : 2 * n + 1]) * stats[2 * n + 1 : 2 * n + 2]
-            scaled = scaled * gains[n : n + 1]
-            act[j, 0:W] = (scaled * jax.nn.sigmoid(scaled)).astype(BF16)
-
-        act_t[...] = lax.dot_general(
-            order, act[...].reshape(T * H * WP, C), (((1,), (1,)), ((), ())),
-            preferred_element_type=F32,
-        ).astype(BF16)
+            act[j, 0:W] = activated(hid[t, h], 1).astype(BF16)
+
+        order = jnp.where(same, 1.0, 0.0).astype(BF16)
+        act_t[...] = turned(order, act[...].reshape(T * H * WP, C))
+
+    def activate_features():
+        @pl.loop(0, 2 * T * (H + 2))
+        def _(j):
+            f, r = j // (H + 2), lax.rem(j, H + 2)
+            inside = jnp.logical_and(
+                jnp.logical_and(jnp.logical_or(r > 0, has_left), jnp.logical_or(r < H + 1, has_right)),
+                jnp.logical_or(f >= T, has_before),
+            )
+            value = activated(wide_feat[f, r], 0)
+            wide_act[f, r, 0:W] = jnp.where(inside, value, 0.0).astype(BF16)
+
+        for b in range(3):
+            cells = wide_act[:, b : b + H].reshape(2 * T * H * WP, C)
+            wide_act_t[b] = turned(perm[...], cells)
 
     def own_row(ref, k):
         return ref[k : k + 1, pl.ds(off, half)]
@@ -498,6 +584,7 @@
     halo_start(0, graw2)
     tmp[...] = jnp.zeros_like(tmp)
     act[...] = jnp.zeros_like(act)
+    wide_act[...] = jnp.zeros_like(wide_act)
     for graw in (graw2, graw1):
         @pl.when(sp == 0)
         def _():
@@ -518,8 +605,9 @@
     perm[...] = jnp.where(cols == source, 1.0, 0.0).astype(BF16)
     same = rows == cols
     block_sum[...] = jnp.where(rows // per == cols // per, 1.0, 0.0).astype(F32)
+    by_rows(feat_n, feat)
+    feature_start()
     by_rows(hid_n, hid)
-    by_rows(feat_n, feat)
 
     def back_parts(kernel, later):
         for f in range(T):
@@ -547,62 +635,69 @@
         stats[2 * n + 1 : 2 * n + 2] = lax.rsqrt(spread + EPS)
     exchange(0).wait_recv()
     reduce_slopes(1, slopes(hid, 1))
-    activate(hid, 1, jnp.where(same, 1.0, 0.0).astype(BF16))
+    activate_hidden()
     for p in range(3):
         delta_part(p)
-        tick(p, 0)
-    activate(feat, 0, perm[...])
+        tick(p, 0, 0)
+        tick(p, 1, 0)
+    feature_wait()
+    activate_features()
     z_to_x(1, zb_b.at[1], xb_b.at[1])
-    ticks(1)
+    ticks(0, 1)
+    ticks(1, 1)
     totals_two = x_total(1, zb_b.at[1], xb_b.at[1])
 
     hidden_rows(totals_two)
     halo_start(1, graw1)
-    ticks(2)
-    halo_wait(1, graw1, (0, 1))
-    shift(graw1, 0, T)
-    delta_part(3)
-    rs_start(3)
+    shift_own(graw1)
+    for p in range(3, 8):
+        delta_part(p)
+        rs_start(p)
+        if p == 3:
+            ticks(0, 2)
+            ticks(1, 2)
     loads[4].wait()
     exchange(0).wait_send()
+    halo_wait(1, graw1, (0, 1))
+    shift_edges(graw1)
+    ticks(0, 3)
     back_parts(k1, False)
-    ticks(3)
+    for p in range(3, 8):
+        rs_pass(p)
     halo_wait(1, graw1, (2, 3, 4))
+    ticks(0, 4)
     shift(graw1, T, 2 * T)
-    for p in range(4, 8):
-        delta_part(p)
-        rs_start(p)
-    rs_pass(3)
-    ticks(4)
     back_parts(k1, True)
     exchange(1).start()
-    rs_pass(4)
-    for p in range(5, 8):
-        rs_pass(p)
-    ticks(5)
+    ticks(1, 3)
+    ticks(0, 5)
+    rs_z1(3)
     exchange(1).wait_recv()
     reduce_slopes(0, slopes(feat, 0))
-    rs_z1(3)
-    ticks(6)
+    ticks(1, 4)
+    ticks(0, 6)
     rs_z1(4)
+    rs_z2(3)
+    ticks(1, 5)
     for p in range(5, 8):
         rs_z1(p)
-    ticks(7)
-    rs_z2(3)
+    ticks(0, 7)
     rs_z2(4)
     z_to_x(2, zb_b.at[0], xb_b.at[0])
+    ticks(1, 6)
     for p in range(5, 8):
         rs_z2(p)
+    feature_rows(x_total(2, zb_b.at[0], xb_b.at[0]))
     for q in range(3):
         ring_pass(q)
-    feature_rows(x_total(2, zb_b.at[0], xb_b.at[0]))
+    for p in range(3, 8):
+        rs_end(p)
     for q in range(3):
         ring_end(q)
-    for p in range(3, 8):
-        rs_end(p)
 
     halo_sent(0, graw2)
     halo_sent(1, graw1)
+    feature_sent()
     reduced_sent(0, zb_a, xb_a)
     reduced_sent(1, zb_b.at[1], xb_b.at[1])
     reduced_sent(2, zb_b.at[0], xb_b.at[0])
@@ -648,7 +743,7 @@
             pltpu.VMEM((T, W, H, C), BF16),
             pltpu.VMEM((T, W, H, C), BF16),
             pltpu.VMEM((T, W, H, C), BF16),
-            pltpu.VMEM((T, H, W, C), BF16),
+            pltpu.VMEM((2 * T, H + 2, W, C), BF16),
             pltpu.VMEM((T, H, W, C), BF16),
             pltpu.VMEM((27, C, half), BF16),
             pltpu.VMEM((27, C, half), BF16),
@@ -660,6 +755,9 @@
             pltpu.VMEM((2 * T, H + 2, WP, 3 * half), BF16),
             pltpu.VMEM((T * H, WP, C), BF16),
             pltpu.VMEM((C, T * H * WP), BF16),
+            pltpu.VMEM((2 * T, H + 2, WP, C), BF16),
+            pltpu.VMEM((3, C, 2 * T * H * WP), BF16),
+            pltpu.VMEM((3, C, wide), F32),
             pltpu.VMEM((C, C), BF16),
             pltpu.VMEM((C, C), F32),
             pltpu.VMEM((C, half), F32),
@@ -685,8 +783,8 @@
             pltpu.VMEM((3, NS, share, wide), BF16),
             pltpu.VMEM((3, NS - 1, share, wide), BF16),
             DMA((5,)),
-            DMA((2, 5)),
-            DMA((2, 5)),
+            DMA((3, 5)),
+            DMA((3, 5)),
             DMA((3, 2)),
             DMA((3, 2)),
             DMA((2,)),

time: 97.8 us -> 94.4 us (0.965)
  Pallas kernels: 97 us -> 93.6 us
    pallas_call x1, Pallas kernels: 95.3 us -> 91.9 us  [shards(): call(by_column(features), by_column(hidden), by_column(cotangent), by_tap...]
where the time goes in v3:
time: 94.4 us; the launch traced here: 94.2 us
  Pallas kernels  93.6 us (99%)
    pallas_call x1, Pallas kernels, shards(): call(by_column(features), by_column(hidden), by_column(cotangent), by_tap...  91.9 us

profile of v3, /device:TPU:40, one launch (start us, length us, event | category | flops | bytes accessed | tf_op | source)
XLA Modules:
  0.0 94.2 jit_solution(13397241321650062843)
XLA Ops:
  0.6 91.9 %block_back.1 = (bf16[2,90,4,128]{3,2,1,0:T(4,128)(2,1)}, f32[27,4,128]{2,1,0:T(4,128)}, f32[27,4,128]{2,1,0:T(4,128)}, f32[2,128]{1,0:T(2,128)}) custom-call(bf16[2,90,4,256]{3,2,1,0:T(4,128)(2,1)} %bitcast.18, bf16[2,90,4,256]{3,2,1,0:T(4,128)(2,1)} %bitcast.19, bf16[2,90,4,256]{3,2,1,0:T(4,128)(2,1)} %bitcast.20, bf16[27,256,128]{2,1,0:T(8,128)(2,1)} %bitcast.16, ...), custom_call_target="tpu_custom_call" | custom-call | tf_op jit(solution)/shard_map/block_back/pallas_call | solution.py:813
  92.6 1.7 %hand_on.1 = (bf16[2,90,4,128]{3,2,1,0:T(4,128)(2,1)}, f32[27,4,128]{2,1,0:T(4,128)}, f32[27,4,128]{2,1,0:T(4,128)}, f32[2,128]{1,0:T(2,128)}) custom-call(bf16[2,90,4,128]{3,2,1,0:T(4,128)(2,1)} %get-tuple-element.12.refs_0_, f32[27,4,128]{2,1,0:T(4,128)} %get-tuple-element.13.refs_1_, f32[27,4,128]{2,1,0:T(4,128)} %get-tuple-element.14.refs_2_, ...), custom_call_target="tpu_custom_call" | custom-call | tf_op jit(solution)/shard_map/hand_on/pallas_call | solution.py:817

commit v4 on v3

--- a/solution.py
+++ b/solution.py
@@ -660,40 +660,41 @@
     exchange(0).wait_send()
     halo_wait(1, graw1, (0, 1))
     shift_edges(graw1)
+    back_parts(k1, False)
+    rs_pass(3)
     ticks(0, 3)
-    back_parts(k1, False)
-    for p in range(3, 8):
+    for p in range(4, 8):
         rs_pass(p)
     halo_wait(1, graw1, (2, 3, 4))
     ticks(0, 4)
+    ticks(1, 3)
     shift(graw1, T, 2 * T)
     back_parts(k1, True)
     exchange(1).start()
-    ticks(1, 3)
+    rs_z1(3)
     ticks(0, 5)
-    rs_z1(3)
+    ticks(1, 4)
     exchange(1).wait_recv()
     reduce_slopes(0, slopes(feat, 0))
-    ticks(1, 4)
+    rs_z1(4)
     ticks(0, 6)
-    rs_z1(4)
+    ticks(1, 5)
     rs_z2(3)
-    ticks(1, 5)
     for p in range(5, 8):
         rs_z1(p)
     ticks(0, 7)
+    ticks(1, 6)
     rs_z2(4)
-    z_to_x(2, zb_b.at[0], xb_b.at[0])
-    ticks(1, 6)
     for p in range(5, 8):
         rs_z2(p)
+    z_to_x(2, zb_b.at[0], xb_b.at[0])
+    for q in range(3):
+        ring_pass(q)
     feature_rows(x_total(2, zb_b.at[0], xb_b.at[0]))
     for q in range(3):
-        ring_pass(q)
+        ring_end(q)
     for p in range(3, 8):
         rs_end(p)
-    for q in range(3):
-        ring_end(q)
 
     halo_sent(0, graw2)
     halo_sent(1, graw1)

time: 94.4 us -> 95.3 us (level)
  no operation moved by 1% of the time
where the time goes in v4:
time: 95.3 us; the launch traced here: 95.2 us
  Pallas kernels  94.5 us (99%)
    pallas_call x1, Pallas kernels, shards(): call(by_column(features), by_column(hidden), by_column(cotangent), by_tap...  92.9 us

profile of v4, /device:TPU:40, one launch (start us, length us, event | category | flops | bytes accessed | tf_op | source)
XLA Modules:
  0.0 95.2 jit_solution(13829670438556654837)
XLA Ops:
  0.6 92.9 %block_back.1 = (bf16[2,90,4,128]{3,2,1,0:T(4,128)(2,1)}, f32[27,4,128]{2,1,0:T(4,128)}, f32[27,4,128]{2,1,0:T(4,128)}, f32[2,128]{1,0:T(2,128)}) custom-call(bf16[2,90,4,256]{3,2,1,0:T(4,128)(2,1)} %bitcast.18, bf16[2,90,4,256]{3,2,1,0:T(4,128)(2,1)} %bitcast.19, bf16[2,90,4,256]{3,2,1,0:T(4,128)(2,1)} %bitcast.20, bf16[27,256,128]{2,1,0:T(8,128)(2,1)} %bitcast.16, ...), custom_call_target="tpu_custom_call" | custom-call | tf_op jit(solution)/shard_map/block_back/pallas_call | solution.py:814
  93.5 1.7 %hand_on.1 = (bf16[2,90,4,128]{3,2,1,0:T(4,128)(2,1)}, f32[27,4,128]{2,1,0:T(4,128)}, f32[27,4,128]{2,1,0:T(4,128)}, f32[2,128]{1,0:T(2,128)}) custom-call(bf16[2,90,4,128]{3,2,1,0:T(4,128)(2,1)} %get-tuple-element.12.refs_0_, f32[27,4,128]{2,1,0:T(4,128)} %get-tuple-element.13.refs_1_, f32[27,4,128]{2,1,0:T(4,128)} %get-tuple-element.14.refs_2_, ...), custom_call_target="tpu_custom_call" | custom-call | tf_op jit(solution)/shard_map/hand_on/pallas_call | solution.py:818

commit v5 on v3

--- a/solution.py
+++ b/solution.py
@@ -289,8 +289,11 @@
             else:
                 acc[k, f * H : (f + 1) * H] += piece
 
-    def exchange(n):
-        return remote(acc.at[1 - ch], acc_in.at[n], ch_s.at[n], ch_r.at[n], {"chan": 1 - ch})
+    def exchange(n, f):
+        part = pl.ds(f * H, H)
+        return remote(
+            acc.at[1 - ch, part], acc_in.at[n, part], ch_s.at[n, f], ch_r.at[n, f], {"chan": 1 - ch}
+        )
 
     def lanes(p):
         q, low, high = PIECES[p]
@@ -609,11 +612,13 @@
     feature_start()
     by_rows(hid_n, hid)
 
-    def back_parts(kernel, later):
+    def back_parts(kernel, later, n=None):
         for f in range(T):
             for a in (2, 1, 0):
                 if (f + 2 - a >= T) == later:
                     back_part(kernel, f, a, a == 2)
+            if later:
+                exchange(n, f).start()
 
     halo_wait(0, graw2, (0, 1))
     shift(graw2, 0, T)
@@ -622,8 +627,7 @@
     z_to_x(0, zb_a, xb_a)
     halo_wait(0, graw2, (2, 3, 4))
     shift(graw2, T, 2 * T)
-    back_parts(k2, True)
-    exchange(0).start()
+    back_parts(k2, True, 0)
     totals = lax.dot_general(
         x_total(0, zb_a, xb_a), spread_sum[...], (((1,), (1,)), ((), ())),
         precision=lax.Precision.HIGHEST, preferred_element_type=F32,
@@ -633,7 +637,8 @@
         spread = totals[2 * n + 1 : 2 * n + 2] - mean * mean
         stats[2 * n : 2 * n + 1] = mean
         stats[2 * n + 1 : 2 * n + 2] = lax.rsqrt(spread + EPS)
-    exchange(0).wait_recv()
+    for f in range(T):
+        exchange(0, f).wait_recv()
     reduce_slopes(1, slopes(hid, 1))
     activate_hidden()
     for p in range(3):
@@ -657,7 +662,8 @@
             ticks(0, 2)
             ticks(1, 2)
     loads[4].wait()
-    exchange(0).wait_send()
+    for f in range(T):
+        exchange(0, f).wait_send()
     halo_wait(1, graw1, (0, 1))
     shift_edges(graw1)
     ticks(0, 3)
@@ -667,12 +673,12 @@
     halo_wait(1, graw1, (2, 3, 4))
     ticks(0, 4)
     shift(graw1, T, 2 * T)
-    back_parts(k1, True)
-    exchange(1).start()
+    back_parts(k1, True, 1)
     ticks(1, 3)
     ticks(0, 5)
     rs_z1(3)
-    exchange(1).wait_recv()
+    for f in range(T):
+        exchange(1, f).wait_recv()
     reduce_slopes(0, slopes(feat, 0))
     ticks(1, 4)
     ticks(0, 6)
@@ -701,7 +707,8 @@
     reduced_sent(0, zb_a, xb_a)
     reduced_sent(1, zb_b.at[1], xb_b.at[1])
     reduced_sent(2, zb_b.at[0], xb_b.at[0])
-    exchange(1).wait_send()
+    for f in range(T):
+        exchange(1, f).wait_send()
     for p in range(3, 8):
         rs_sent(p)
     for q in range(3):
@@ -787,8 +794,8 @@
             DMA((3, 5)),
             DMA((3, 2)),
             DMA((3, 2)),
-            DMA((2,)),
-            DMA((2,)),
+            DMA((2, T)),
+            DMA((2, T)),
             DMA((8, 2)),
             DMA((8, 2)),
             DMA((8, 2)),

time: 94.4 us -> 94.1 us (level)
  no operation moved by 1% of the time
where the time goes in v5:
time: 94.1 us; the launch traced here: 94 us
  Pallas kernels  93.3 us (99%)
    pallas_call x1, Pallas kernels, shards(): call(by_column(features), by_column(hidden), by_column(cotangent), by_tap...  91.7 us

profile of v5, /device:TPU:40, one launch (start us, length us, event | category | flops | bytes accessed | tf_op | source)
XLA Modules:
  0.0 94.0 jit_solution(16961544665138180776)
XLA Ops:
  0.6 91.7 %block_back.1 = (bf16[2,90,4,128]{3,2,1,0:T(4,128)(2,1)}, f32[27,4,128]{2,1,0:T(4,128)}, f32[27,4,128]{2,1,0:T(4,128)}, f32[2,128]{1,0:T(2,128)}) custom-call(bf16[2,90,4,256]{3,2,1,0:T(4,128)(2,1)} %bitcast.18, bf16[2,90,4,256]{3,2,1,0:T(4,128)(2,1)} %bitcast.19, bf16[2,90,4,256]{3,2,1,0:T(4,128)(2,1)} %bitcast.20, bf16[27,256,128]{2,1,0:T(8,128)(2,1)} %bitcast.16, ...), custom_call_target="tpu_custom_call" | custom-call | tf_op jit(solution)/shard_map/block_back/pallas_call | solution.py:820
  92.3 1.7 %hand_on.1 = (bf16[2,90,4,128]{3,2,1,0:T(4,128)(2,1)}, f32[27,4,128]{2,1,0:T(4,128)}, f32[27,4,128]{2,1,0:T(4,128)}, f32[2,128]{1,0:T(2,128)}) custom-call(bf16[2,90,4,128]{3,2,1,0:T(4,128)(2,1)} %get-tuple-element.12.refs_0_, f32[27,4,128]{2,1,0:T(4,128)} %get-tuple-element.13.refs_1_, f32[27,4,128]{2,1,0:T(4,128)} %get-tuple-element.14.refs_2_, ...), custom_call_target="tpu_custom_call" | custom-call | tf_op jit(solution)/shard_map/hand_on/pallas_call | solution.py:824
